TPU v7x, 512 devices: a 8x2x16 block of a 8x8x16 slice. The times are simulated.
512 devices in a mesh: prompt: 2 (over y), seq: 16 (over z), blk: 8 (over x), cfg: 2 (over core).
Axes of the slice: x: 8, y: 2, z: 16, core: 2. Of those that a mesh axis runs over, the one named last changes fastest.
The devices are a block of a 8x8x16 slice.
Arguments:
- queries: bfloat16 [2, 12288, 4096], P('cfg', ('prompt', 'blk', 'seq')), parts along dimension 1, may hold values from -5 to 5
- key_states: bfloat16 [2, 12288, 4096], P('cfg', ('prompt', 'blk', 'seq')), parts along dimension 1, may hold values from -5 to 5
- value_states: bfloat16 [2, 12288, 4096], P('cfg', ('prompt', 'blk', 'seq')), parts along dimension 1, may hold values from -6 to 6
- noisy_latents: float32 [12288, 64], P(('prompt', 'blk', 'seq')), parts along dimension 0, may hold values from -6 to 6
- patch_order: int32 [12288], P(('prompt', 'blk', 'seq')), parts along dimension 0, may hold values from 0 to 6143, as said below
- head_weight: bfloat16 [4096, 64], replicated, may hold values from -0.75 to 0.75
- latent_std: float32 [16], replicated, may hold values from 0.1 to 1.9
- latent_mean: float32 [16], replicated, may hold values from -3 to 3
- conv_weight: bfloat16 [3, 3, 3, 16, 384], replicated, may hold values from -0.3125 to 0.3125
- conv_bias: float32 [384], replicated, may hold values from -2 to 2
Outputs:
- features: bfloat16 [16, 64, 48, 384], P(('prompt', 'cfg'), 'seq', 'blk'), parts along dimension 0
There are 2 independent parts, one for each index of `prompt`. A program takes and returns all parts, laid end to end along the dimension named above; an argument that names none is the same for every part. Nothing has to cross between parts.
Inputs may be any that keep to these rules, and one draw needn't show every extreme that they name: A permutation of 0 to 6143 that keeps every aligned block of 48 tokens within itself: patch_order[t] // 48 == t // 48.
All inputs are finite; a program needn't handle non-finite values.
Results may differ from a plain program's by a relative error of at most 0.012.
Values may be sent and summed in bfloat16 or wider, within the bound.
A program may use at most 128 MiB of HBM per device.

v0:
```python
import functools
import math

import jax
import jax.numpy as jnp
from jax import lax
from jax.experimental import pallas as pl
from jax.experimental.pallas import tpu as pltpu
from jax.sharding import PartitionSpec as P

HDIM = 128
ZCH = 16
COLS_DEV = 3
ROW_PAD = 8
TAP_LANES = 256
ONES = 16
GUIDE = 5.0
NOISE_LEVEL = 0.5
MESH = pl.DeviceIdType.MESH
BEGIN, QUERIES, PASS, ATTEND = range(4)
BOTH = 2
ORDER = (
    (BEGIN, 0, 0), (PASS, 0, 1, 0, BOTH), (BEGIN, 0, 1), (PASS, 0, 2, 0, BOTH), (BEGIN, 1, 0),
    (PASS, 0, 1, 1, BOTH), (PASS, 0, 3, 0, BOTH), (PASS, 1, 1, 0, BOTH), (BEGIN, 1, 1),
    (PASS, 0, 2, 1, BOTH), (PASS, 0, 4, 0, 0), (PASS, 1, 2, 0, BOTH), (PASS, 1, 1, 1, BOTH),
    (PASS, 0, 3, 1, 1), (QUERIES, 0), (ATTEND, 0, 0), (PASS, 0, 3, 1, 0), (PASS, 1, 3, 0, 1),
    (ATTEND, 0, -1), (ATTEND, 0, 1), (BEGIN, 2, 0), (PASS, 1, 3, 0, 0), (PASS, 1, 2, 1, 1),
    (ATTEND, 0, 2), (PASS, 1, 2, 1, 0), (PASS, 0, 4, 1, 1), (ATTEND, 0, -2), (PASS, 2, 1, 0, BOTH),
    (BEGIN, 2, 1), (PASS, 1, 4, 0, 0), (PASS, 1, 3, 1, 1), (ATTEND, 0, 3), (PASS, 1, 3, 1, 0),
    (PASS, 2, 2, 0, 1), (ATTEND, 0, -3), (PASS, 2, 2, 0, 0), (PASS, 2, 1, 1, BOTH),
    (PASS, 1, 4, 1, 1), (ATTEND, 0, 4), (QUERIES, 1), (ATTEND, 1, 0), (PASS, 2, 3, 0, BOTH),
    (ATTEND, 1, -1), (ATTEND, 1, 1), (PASS, 2, 2, 1, BOTH), (ATTEND, 1, -2), (ATTEND, 1, 2),
    (PASS, 2, 4, 0, 0), (PASS, 2, 3, 1, BOTH), (ATTEND, 1, -3), (ATTEND, 1, 3), (PASS, 2, 4, 1, 1),
    (ATTEND, 1, 4),
)
EXP_SCALE = math.log2(math.e) / math.sqrt(HDIM)


def exchange_kernel(
    nz, nx, q_hbm, k_hbm, v_hbm, w_hbm, taps_hbm, noisy_ref, order_ref, std_ref, mean_ref, out_ref,
    q_ref, k_ref, v_ref, w_ref, taps_ref,
    vsend, gx, qx, vt, top, acc, wide, vout, vin, psend, tile, halo, grid, xcol, wexp, final,
    zsend, zrecv, xsend, xrecv, vsent, vrecv, psent, precv, loaded,
):
    seq = lax.axis_index("seq")
    blk = lax.axis_index("blk")
    cfg = lax.axis_index("cfg")
    tok = q_ref.shape[0]
    rows = gx.shape[2]
    part = rows // 2
    patch = w_ref.shape[0]
    frames = nx // 2
    few = tok // 2
    hops = nx // 2
    right = lax.rem(blk + 1, nx)
    left = lax.rem(blk + nx - 1, nx)

    barrier = pltpu.get_barrier_semaphore()

    loads = [
        pltpu.make_async_copy(there, here, loaded.at[n])
        for n, (there, here) in enumerate(
            ((k_hbm, k_ref), (v_hbm, v_ref), (w_hbm, w_ref), (q_hbm, q_ref), (taps_hbm, taps_ref))
        )
    ]
    for load in loads:
        load.start()

    def peer_at(d):
        far = nz // 2 - d // 2
        return lax.rem(seq + jnp.where(lax.rem(d, 2) == 1, far, nz - far), nz)

    def greet(d, _):
        pl.semaphore_signal(barrier, inc=1, device_id={"seq": peer_at(d)}, device_id_type=MESH)
        return 0

    lax.fori_loop(1, nz, greet, 0)
    for there in ({"blk": left}, {"blk": right}, {"cfg": 1 - cfg}):
        pl.semaphore_signal(barrier, inc=1, device_id=there, device_id_type=MESH)
    loads[0].wait()
    pl.semaphore_wait(barrier, nz + 2)

    def project(s, _):
        both = []
        for h in range(2):
            at = pl.ds(pl.multiple_of((2 * s + h) * HDIM, HDIM), HDIM)
            both.append(
                lax.dot_general(
                    v_ref[:, at], w_ref[:, at], (((1,), (1,)), ((), ())),
                    preferred_element_type=jnp.float32,
                )
            )
        vsend[s] = jnp.concatenate(both, axis=1).astype(jnp.bfloat16)
        return 0

    def columns(ref, first, count, s, h):
        return ref.at[pl.ds(first, count), pl.ds(pl.multiple_of((2 * s + h) * HDIM, HDIM), HDIM)]

    def source_place(n):
        return lax.rem(seq + jnp.where(lax.rem(n, 2) == 1, nz - (n + 1) // 2, n // 2), nz)

    def half_of(c, half):
        source = (lambda s: vsend.at[s]) if c == 1 else (lambda s: columns(k_ref, 0, tok, s, c // 2))
        return source, gx.at[c, blk, pl.ds(half * part, part), :], half

    def query_of(h):
        return lambda s: columns(q_ref, 0, tok, s, h), qx.at[h], None

    parcels = (
        half_of(0, 0), half_of(0, 1), half_of(1, 0), half_of(1, 1), query_of(0),
        half_of(2, 0), half_of(2, 1), query_of(1),
    )

    def spread(i):
        source, whole, half = parcels[i]

        def there(place):
            return whole.at[pl.ds(pl.multiple_of(place * tok, 16), tok), :]

        if half != 1:
            own = there(seq if half is None else 0)
            pltpu.make_async_copy(source(seq), own, zrecv.at[i]).start()

        def send(d, _):
            n = nz - d
            peer = source_place(n) if half is not None else peer_at(d)
            pltpu.make_async_remote_copy(
                src_ref=source(peer),
                dst_ref=there(seq if half is None else n - half * (nz // 2)),
                send_sem=zsend.at[i],
                recv_sem=zrecv.at[i],
                device_id={"seq": peer},
                device_id_type=MESH,
            ).start()
            return 0

        first, last = {None: (1, nz), 0: (nz // 2 + 1, nz), 1: (1, nz // 2 + 1)}[half]
        lax.fori_loop(first, last, send, 0)

    def spread_done(i):
        whole = parcels[i][1]
        pltpu.make_async_copy(whole, whole, zrecv.at[i]).wait()

    def ring(c, way, step, half):
        block = lax.rem(blk + (nx - step + 1 if way == 0 else step - 1), nx)
        piece = gx.at[c, block, pl.ds(half * part, part), :]
        return pltpu.make_async_remote_copy(
            src_ref=piece,
            dst_ref=piece,
            send_sem=xsend.at[c, way, step - 1, half],
            recv_sem=xrecv.at[c, way, step - 1, half],
            device_id={"blk": right if way == 0 else left},
            device_id_type=MESH,
        )

    def travels(way, step, half):
        return step < hops or (step == hops and way == half)

    def begin(c, half):
        for way in range(2):
            if travels(way, 1, half):
                ring(c, way, 1, half).start()

    def advance(c, step, half, way):
        if travels(way, step, half):
            ring(c, way, step, half).wait_recv()
            if travels(way, step + 1, half):
                ring(c, way, step + 1, half).start()

    qtile = rows // 2

    def attend(h, blocks):
        if h == 0:
            for block in blocks:
                turned = gx[1, block].T
                for g in range(2):
                    vt[block, g, pl.ds(0, patch), :] = turned[g * patch : (g + 1) * patch, :]
        items = [(block, t) for block in blocks for t in range(rows // qtile)]

        def scores_of(block, t):
            return lax.dot_general(
                gx[2 * h, block], qx[h, pl.ds(t * qtile, qtile), :], (((1,), (1,)), ((), ())),
                preferred_element_type=jnp.float32,
            )

        ahead = len(blocks)
        ready = [scores_of(*item) for item in items[:ahead]]
        for n, (block, t) in enumerate(items):
            if n + ahead < len(items):
                ready.append(scores_of(*items[n + ahead]))
            scores = ready.pop(0)
            at = pl.ds(t * qtile, qtile)
            old = top[h, :, at]
            new = jnp.maximum(old, jnp.max(scores, axis=0, keepdims=True))
            expo = jnp.exp2(scores * EXP_SCALE - new * EXP_SCALE).astype(jnp.bfloat16)
            factor = jnp.exp2((old - new) * EXP_SCALE)
            top[h, :, at] = new
            acc[h, :, at] = acc[h, :, at] * factor + jnp.dot(
                vt[block, h], expo, preferred_element_type=jnp.float32
            )

    spread(0)
    spread(1)
    loads[1].wait()
    loads[2].wait()
    lax.fori_loop(0, nz, project, 0)
    loads[3].wait()
    for i in range(2, len(parcels)):
        spread(i)
    top[...] = jnp.full(top.shape, -1e30, jnp.float32)
    acc[...] = jnp.zeros(acc.shape, jnp.float32)
    vt[:, :, pl.ds(patch, vt.shape[2] - patch), :] = jnp.ones(
        (nx, 2, vt.shape[2] - patch, rows), jnp.bfloat16
    )
    xcol[...] = jnp.zeros(xcol.shape, jnp.float32)
    loads[4].wait()
    wexp[...] = jnp.zeros(wexp.shape, jnp.bfloat16)
    for step_t in range(3):
        for step_y in range(3):
            taps = taps_ref[pl.ds((3 * step_t + step_y) * 3 * ZCH, 3 * ZCH), :]
            at = step_t * TAP_LANES + step_y * 4 * ZCH
            wexp[0, pl.ds(at + ZCH, 3 * ZCH), :] = taps
            wexp[1, pl.ds(at, 3 * ZCH), :] = taps

    for kind, c, *rest in ORDER:
        if kind == BEGIN:
            spread_done(((0, 1), (2, 3), (5, 6))[c][rest[0]])
            begin(c, rest[0])
        elif kind == QUERIES:
            spread_done((4, 7)[c])
        elif kind == PASS:
            step, half, way = rest
            for one in (0, 1) if way == BOTH else (way,):
                advance(c, step, half, one)
        else:
            attend(c, [lax.rem(blk + nx + rest[0], nx)])

    velocity = 0.0
    for h in range(2):
        velocity = velocity + acc[h, pl.ds(0, patch), :] / acc[h, pl.ds(patch, 1), :]
    velocity = velocity * jnp.where(cfg == 0, GUIDE, 1.0 - GUIDE)
    later = pltpu.roll(velocity, rows - few, 1)
    wide[...] = jnp.concatenate([velocity, later], axis=0).T

    def pack(s, _):
        vout[s] = wide[pl.ds(pl.multiple_of(s * tok, 16), few), :].astype(jnp.bfloat16)
        return 0

    lax.fori_loop(0, nz, pack, 0)
    slot = cfg * nz + seq

    def share(peer):
        return pltpu.make_async_remote_copy(
            src_ref=vout.at[peer],
            dst_ref=vin.at[slot],
            send_sem=vsent,
            recv_sem=vrecv,
            device_id={"seq": peer, "cfg": 1},
            device_id_type=MESH,
        )

    def send_share(d, _):
        share(peer_at(d)).start()
        return 0

    lax.fori_loop(1, nz, send_share, 0)

    @pl.when(cfg == 0)
    def _():
        share(seq).start()
        pltpu.make_async_copy(vout, vout, vsent).wait()

    def greater(target_cfg):
        return blk < frames if target_cfg == 0 else blk >= frames - 2

    @pl.when(cfg == 1)
    def _():
        pltpu.make_async_copy(vout.at[seq], vin.at[slot], vrecv).start()
        pltpu.make_async_copy(vin, vin, vrecv).wait()
        guided = jnp.sum(vin[...].astype(jnp.float32), axis=0)
        noisy = jnp.concatenate([noisy_ref[0:few, :], noisy_ref[few:tok, :]], axis=1)
        scale = jnp.concatenate([std_ref[...]] * (2 * patch // ZCH), axis=1)
        shift = jnp.concatenate([mean_ref[...]] * (2 * patch // ZCH), axis=1)
        pixels = (noisy - NOISE_LEVEL * guided) * scale + shift
        pixels = jnp.concatenate([pixels[:, :patch], pixels[:, patch:]], axis=0).astype(jnp.bfloat16)

        entry = lax.broadcasted_iota(jnp.int32, (patch, 2 * patch), 0)
        lane = lax.broadcasted_iota(jnp.int32, (patch, 2 * patch), 1)
        half = patch // 2
        spread_pixels = []
        for p in range(2):
            place = (
                (entry // half == lane // patch)
                & (entry % half == lane % half)
                & ((lane // half) % 2 == p)
            ).astype(jnp.bfloat16)
            spread_pixels.append(jnp.dot(pixels, place, preferred_element_type=jnp.float32))
        spread_pixels = jnp.concatenate(spread_pixels, axis=0).astype(jnp.bfloat16)
        slots = order_ref[...] - (blk * nz + seq) * tok
        slots = jnp.concatenate([slots, slots], axis=1)
        row = lax.broadcasted_iota(jnp.int32, (ROW_PAD * nx, 2 * tok), 0)
        token = lax.broadcasted_iota(jnp.int32, (ROW_PAD * nx, 2 * tok), 1)
        x = row % ROW_PAD
        column = COLS_DEV * (row // ROW_PAD) - 1 + (x + 1) // 2 + token // tok
        inside = (x < 2 * COLS_DEV) & (column >= 0) & (column < COLS_DEV * nx)
        for i in range(2):
            select = (inside & (slots == column + i * COLS_DEV * nx)).astype(jnp.bfloat16)
            picked = jnp.dot(select, spread_pixels, preferred_element_type=jnp.float32)
            psend[:, :, i * 2 * patch : (i + 1) * 2 * patch] = picked.reshape(
                nx, ROW_PAD, 2 * patch
            ).astype(jnp.bfloat16)

        above = lax.rem(seq + nz - 1, nz)
        below = lax.rem(seq + 1, nz)
        pieces = (
            (1, pl.ds(2 * patch, 2 * patch), halo.at[blk, 0], below),
            (1, pl.ds(0, 2 * patch), halo.at[blk, 1], above),
            (0, pl.ds(0, 4 * patch), tile.at[blk], seq),
        )
        for c in range(2):

            @pl.when(greater(c))
            def _():
                def send_pieces(d, _):
                    far = nx // 2 - d // 2
                    b = lax.rem(blk + jnp.where(lax.rem(d, 2) == 1, far, nx - far), nx)
                    for kind, at, there, s in pieces:
                        pltpu.make_async_remote_copy(
                            src_ref=psend.at[b, :, at],
                            dst_ref=there,
                            send_sem=psent.at[c, kind],
                            recv_sem=precv.at[kind],
                            device_id={"seq": s, "blk": b, "cfg": c},
                            device_id_type=MESH,
                        ).start()
                    return 0

                lax.fori_loop(1, nx, send_pieces, 0)
                for kind, at, there, s in pieces:
                    if c == 1 and kind == 0:
                        pltpu.make_async_copy(psend.at[blk, :, at], there, precv.at[0]).start()
                    else:
                        pltpu.make_async_remote_copy(
                            src_ref=psend.at[blk, :, at],
                            dst_ref=there,
                            send_sem=psent.at[c, kind],
                            recv_sem=precv.at[kind],
                            device_id={"seq": s, "cfg": c},
                            device_id_type=MESH,
                        ).start()

    for c in range(2):

        @pl.when(cfg == c)
        def _():
            arrived = pl.ds(0, frames) if c == 0 else pl.ds(frames - 2, frames + 2)
            pltpu.make_async_copy(tile.at[arrived], tile.at[arrived], precv.at[0]).wait()
            pltpu.make_async_copy(halo.at[arrived], halo.at[arrived], precv.at[1]).wait()

    def line(g, _):
        frame = cfg * frames - 2 + g
        known = frame >= 0
        frame = jnp.maximum(frame, 0)
        upper = halo[frame, 0].astype(jnp.float32)[:, patch:]
        lower = halo[frame, 1].astype(jnp.float32)[:, :patch]
        upper = jnp.where(known & (seq > 0), upper, 0.0)
        lower = jnp.where(known & (seq < nz - 1), lower, 0.0)
        middle = jnp.where(known, tile[frame].astype(jnp.float32), 0.0)
        grid[g] = jnp.concatenate([upper, middle, lower], axis=1)
        return 0

    lax.fori_loop(0, frames + 2, line, 0)
    for f in range(frames):
        for y in range(4):
            for step_t in range(3):
                xcol[pl.ds((4 * f + y) * ROW_PAD, ROW_PAD), pl.ds(step_t * TAP_LANES, 3 * patch)] = grid[
                    f + step_t, :, pl.ds(y * patch, 3 * patch)
                ]
    odd = lax.broadcasted_iota(jnp.int32, xcol.shape, 0) % 2 == 1
    features = 0.0
    for parity in range(2):
        kept = jnp.where(odd if parity else ~odd, xcol[...], 0.0).astype(jnp.bfloat16)
        features = features + jnp.dot(kept, wexp[parity], preferred_element_type=jnp.float32)
    wide_x = 2 * COLS_DEV
    to = lax.broadcasted_iota(jnp.int32, (frames * wide_x * 4, xcol.shape[0]), 0)
    at = lax.broadcasted_iota(jnp.int32, (frames * wide_x * 4, xcol.shape[0]), 1)
    source = ((to // (4 * wide_x)) * 4 + to % 4) * ROW_PAD + (to // 4) % wide_x
    order = (source == at).astype(jnp.bfloat16)
    upper = features.astype(jnp.bfloat16)
    lower = (features - upper.astype(jnp.float32)).astype(jnp.bfloat16)
    final[...] = jnp.dot(order, upper, preferred_element_type=jnp.float32) + jnp.dot(
        order, lower, preferred_element_type=jnp.float32
    )
    for f in range(frames):
        for x in range(wide_x):
            out_ref[f, x] = final[pl.ds((f * wide_x + x) * 4, 4), :]

    @pl.when(cfg == 1)
    def _():
        sent = vout.at[pl.ds(0, nz - 1)]
        pltpu.make_async_copy(sent, sent, vsent).wait()
        for c in range(2):

            @pl.when(greater(c))
            def _():
                tiles = psend.at[pl.ds(0, nx - c)]
                pltpu.make_async_copy(tiles, tiles, psent.at[c, 0]).wait()
                pltpu.make_async_copy(psend, psend, psent.at[c, 1]).wait()

    for i, (_, whole, half) in enumerate(parcels):
        sent = whole if half == 1 else whole.at[pl.ds(0, whole.shape[0] - tok), :]
        pltpu.make_async_copy(sent, sent, zsend.at[i]).wait()
    for c in range(3):
        for step in range(1, hops + 1):
            for half in range(2):
                for way in range(2):
                    if travels(way, step, half):
                        ring(c, way, step, half).wait_send()


def local(
    queries,
    key_states,
    value_states,
    noisy_latents,
    patch_order,
    head_weight,
    latent_std,
    latent_mean,
    conv_weight,
    conv_bias,
):
    nz = lax.axis_size("seq")
    nx = lax.axis_size("blk")
    tok = queries.shape[1]
    rows = nz * tok
    patch = head_weight.shape[1]
    wide = conv_weight.shape[4]
    frames = nx // 2
    pixels = 4 * frames * ROW_PAD
    vmem = pl.BlockSpec(memory_space=pltpu.VMEM)
    features = pl.pallas_call(
        functools.partial(exchange_kernel, nz, nx),
        out_shape=jax.ShapeDtypeStruct((frames, 2 * COLS_DEV, 4, wide), jnp.float32),
        in_specs=[pl.BlockSpec(memory_space=pl.ANY)] * 5 + [vmem] * 4,
        out_specs=vmem,
        scratch_shapes=[
            pltpu.VMEM(queries.shape[1:], jnp.bfloat16),
            pltpu.VMEM(queries.shape[1:], jnp.bfloat16),
            pltpu.VMEM(queries.shape[1:], jnp.bfloat16),
            pltpu.VMEM((patch, head_weight.shape[0]), jnp.bfloat16),
            pltpu.VMEM((27 * ZCH, wide), jnp.bfloat16),
            pltpu.VMEM((nz, tok, 2 * patch), jnp.bfloat16),
            pltpu.VMEM((3, nx, rows, HDIM), jnp.bfloat16),
            pltpu.VMEM((2, rows, HDIM), jnp.bfloat16),
            pltpu.VMEM((nx, 2, patch + ONES, rows), jnp.bfloat16),
            pltpu.VMEM((2, 1, rows), jnp.float32),
            pltpu.VMEM((2, patch + ONES, rows), jnp.float32),
            pltpu.VMEM((rows, 2 * patch), jnp.float32),
            pltpu.VMEM((nz, tok // 2, 2 * patch), jnp.bfloat16),
            pltpu.VMEM((2 * nz, tok // 2, 2 * patch), jnp.bfloat16),
            pltpu.VMEM((nx, ROW_PAD, 4 * patch), jnp.bfloat16),
            pltpu.VMEM((nx, ROW_PAD, 4 * patch), jnp.bfloat16),
            pltpu.VMEM((nx, 2, ROW_PAD, 2 * patch), jnp.bfloat16),
            pltpu.VMEM((frames + 2, ROW_PAD, 6 * patch), jnp.float32),
            pltpu.VMEM((pixels, 3 * TAP_LANES), jnp.float32),
            pltpu.VMEM((2, 3 * TAP_LANES, wide), jnp.bfloat16),
            pltpu.VMEM((8 * frames * COLS_DEV, wide), jnp.float32),
            pltpu.SemaphoreType.DMA((8,)),
            pltpu.SemaphoreType.DMA((8,)),
            pltpu.SemaphoreType.DMA((3, 2, nx // 2, 2)),
            pltpu.SemaphoreType.DMA((3, 2, nx // 2, 2)),
            pltpu.SemaphoreType.DMA,
            pltpu.SemaphoreType.DMA,
            pltpu.SemaphoreType.DMA((2, 2)),
            pltpu.SemaphoreType.DMA((2,)),
            pltpu.SemaphoreType.DMA((5,)),
        ],
        compiler_params=pltpu.CompilerParams(collective_id=0, has_side_effects=True),
    )(
        queries[0],
        key_states[0],
        value_states[0],
        head_weight.T,
        conv_weight.reshape(27 * ZCH, wide),
        noisy_latents,
        patch_order.reshape(1, tok),
        latent_std.reshape(1, ZCH),
        latent_mean.reshape(1, ZCH),
    )
    return (features + conv_bias).astype(jnp.bfloat16).transpose(0, 2, 1, 3)


def solution(mesh):
    in_specs = (
        P("cfg", ("prompt", "blk", "seq"), None),
        P("cfg", ("prompt", "blk", "seq"), None),
        P("cfg", ("prompt", "blk", "seq"), None),
        P(("prompt", "blk", "seq"), None),
        P(("prompt", "blk", "seq")),
        P(),
        P(),
        P(),
        P(),
        P(),
    )
    out_specs = P(("prompt", "cfg"), "seq", "blk", None)
    return jax.shard_map(local, mesh=mesh, in_specs=in_specs, out_specs=out_specs, check_vma=False)
```

profile of v0, /device:TPU:65, one launch (start us, length us, event | category | flops | bytes accessed | tf_op | source)
XLA Modules:
  0.0 129.7 jit_solution(7217435520092851303)
XLA Ops:
  0.0 0.0 copy-start
  0.0 128.1 %shard_map.100 = f32[4,6,4,384]{3,2,1,0:T(4,128)} custom-call(bf16[48,4096]{1,0:T(8,128)(2,1)} %bitcast.11, bf16[48,4096]{1,0:T(8,128)(2,1)} %bitcast.12, bf16[48,4096]{1,0:T(8,128)(2,1)} %bitcast.13, bf16[64,4096]{1,0:T(8,128)(2,1)} %bitcast.10, bf16[432,384]{1,0:T(8,128)(2,1)} %bitcast.14, f32[48,64]{1,0:T(8,128)} %noisy_ref.1, s32[1,48]{1,0:T(1,128)} %bitcast.15, ...), custom_call_target="tpu_custom_call" | custom-call | tf_op jit(solution)/shard_map/pallas_call | solution.py:442
  128.1 0.0 copy-done
  128.1 1.6 %fusion = bf16[4,4,6,384]{3,1,2,0:T(4,128)(2,1)} fusion(f32[4,6,4,384]{3,2,1,0:T(4,128)} %shard_map.100, f32[384]{0:T(512)S(1)} %copy-done), kind=kLoop, calls=%fused_computation.1 | loop fusion | flops 73728 | bytes 222720 | tf_op jit(solution)/shard_map/transpose | solution.py:491
Async XLA Ops:
  0.0 128.1 %copy-start = (f32[384]{0:T(512)S(1)}, f32[384]{0:T(512)}, u32[]{:S(2)}) copy-start(f32[384]{0:T(512)} %param.19) | copy-start | bytes 4612
where the time goes:
time: 130 us
  Pallas kernels  128 us (98%)
  other arithmetic  1.57 us (1%)
    pallas_call x1, Pallas kernels, local(): pl.pallas_call(functools.partial(exchange_kernel, nz, nx), out_shape=jax....  128 us

commit v1 on v0

--- a/solution.py
+++ b/solution.py
@@ -14,6 +14,7 @@
 ROW_PAD = 8
 TAP_LANES = 256
 ONES = 16
+SPLIT = 2
 GUIDE = 5.0
 NOISE_LEVEL = 0.5
 MESH = pl.DeviceIdType.MESH
@@ -22,15 +23,15 @@
 ORDER = (
     (BEGIN, 0, 0), (PASS, 0, 1, 0, BOTH), (BEGIN, 0, 1), (PASS, 0, 2, 0, BOTH), (BEGIN, 1, 0),
     (PASS, 0, 1, 1, BOTH), (PASS, 0, 3, 0, BOTH), (PASS, 1, 1, 0, BOTH), (BEGIN, 1, 1),
-    (PASS, 0, 2, 1, BOTH), (PASS, 0, 4, 0, 0), (PASS, 1, 2, 0, BOTH), (PASS, 1, 1, 1, BOTH),
-    (PASS, 0, 3, 1, 1), (QUERIES, 0), (ATTEND, 0, 0), (PASS, 0, 3, 1, 0), (PASS, 1, 3, 0, 1),
-    (ATTEND, 0, -1), (ATTEND, 0, 1), (BEGIN, 2, 0), (PASS, 1, 3, 0, 0), (PASS, 1, 2, 1, 1),
-    (ATTEND, 0, 2), (PASS, 1, 2, 1, 0), (PASS, 0, 4, 1, 1), (ATTEND, 0, -2), (PASS, 2, 1, 0, BOTH),
-    (BEGIN, 2, 1), (PASS, 1, 4, 0, 0), (PASS, 1, 3, 1, 1), (ATTEND, 0, 3), (PASS, 1, 3, 1, 0),
-    (PASS, 2, 2, 0, 1), (ATTEND, 0, -3), (PASS, 2, 2, 0, 0), (PASS, 2, 1, 1, BOTH),
-    (PASS, 1, 4, 1, 1), (ATTEND, 0, 4), (QUERIES, 1), (ATTEND, 1, 0), (PASS, 2, 3, 0, BOTH),
-    (ATTEND, 1, -1), (ATTEND, 1, 1), (PASS, 2, 2, 1, BOTH), (ATTEND, 1, -2), (ATTEND, 1, 2),
-    (PASS, 2, 4, 0, 0), (PASS, 2, 3, 1, BOTH), (ATTEND, 1, -3), (ATTEND, 1, 3), (PASS, 2, 4, 1, 1),
+    (PASS, 0, 2, 1, BOTH), (BEGIN, 2, 0), (PASS, 0, 4, 0, 0), (PASS, 1, 2, 0, BOTH),
+    (PASS, 1, 1, 1, BOTH), (PASS, 0, 3, 1, 1), (BEGIN, 2, 1), (PASS, 0, 3, 1, 0),
+    (PASS, 2, 1, 0, BOTH), (PASS, 1, 3, 0, BOTH), (PASS, 1, 2, 1, BOTH), (PASS, 0, 4, 1, 1),
+    (QUERIES, 0), (ATTEND, 0, 0), (PASS, 2, 1, 1, BOTH), (ATTEND, 0, -1), (ATTEND, 0, 1),
+    (PASS, 2, 2, 0, BOTH), (ATTEND, 0, -2), (ATTEND, 0, 2), (PASS, 1, 4, 0, 0), (PASS, 1, 3, 1, 1),
+    (ATTEND, 0, 3), (PASS, 1, 3, 1, 0), (PASS, 2, 2, 1, 1), (ATTEND, 0, -3), (QUERIES, 1),
+    (ATTEND, 1, 0), (PASS, 2, 2, 1, 0), (PASS, 2, 3, 0, 1), (ATTEND, 1, -1), (ATTEND, 1, 1),
+    (PASS, 2, 3, 0, 0), (PASS, 1, 4, 1, 1), (ATTEND, 0, 4), (ATTEND, 1, -2), (PASS, 2, 3, 1, BOTH),
+    (ATTEND, 1, 2), (ATTEND, 1, -3), (PASS, 2, 4, 0, 0), (ATTEND, 1, 3), (PASS, 2, 4, 1, 1),
     (ATTEND, 1, 4),
 )
 EXP_SCALE = math.log2(math.e) / math.sqrt(HDIM)
@@ -107,8 +108,8 @@
         return lambda s: columns(q_ref, 0, tok, s, h), qx.at[h], None
 
     parcels = (
-        half_of(0, 0), half_of(0, 1), half_of(1, 0), half_of(1, 1), query_of(0),
-        half_of(2, 0), half_of(2, 1), query_of(1),
+        half_of(0, 0), half_of(0, 1), half_of(1, 0), half_of(1, 1),
+        half_of(2, 0), half_of(2, 1), query_of(0), query_of(1),
     )
 
     def spread(i):
@@ -141,14 +142,16 @@
         whole = parcels[i][1]
         pltpu.make_async_copy(whole, whole, zrecv.at[i]).wait()
 
-    def ring(c, way, step, half):
+    def ring(c, way, step, half, piece):
         block = lax.rem(blk + (nx - step + 1 if way == 0 else step - 1), nx)
-        piece = gx.at[c, block, pl.ds(half * part, part), :]
+        count = part // SPLIT
+        slot = half * SPLIT + piece
+        moved = gx.at[c, block, pl.ds(slot * count, count), :]
         return pltpu.make_async_remote_copy(
-            src_ref=piece,
-            dst_ref=piece,
-            send_sem=xsend.at[c, way, step - 1, half],
-            recv_sem=xrecv.at[c, way, step - 1, half],
+            src_ref=moved,
+            dst_ref=moved,
+            send_sem=xsend.at[c, way, step - 1, slot],
+            recv_sem=xrecv.at[c, way, step - 1, slot],
             device_id={"blk": right if way == 0 else left},
             device_id_type=MESH,
         )
@@ -157,15 +160,18 @@
         return step < hops or (step == hops and way == half)
 
     def begin(c, half):
-        for way in range(2):
-            if travels(way, 1, half):
-                ring(c, way, 1, half).start()
-
-    def advance(c, step, half, way):
-        if travels(way, step, half):
-            ring(c, way, step, half).wait_recv()
-            if travels(way, step + 1, half):
-                ring(c, way, step + 1, half).start()
+        for piece in range(SPLIT):
+            for way in range(2):
+                if travels(way, 1, half):
+                    ring(c, way, 1, half, piece).start()
+
+    def advance(c, step, half, ways):
+        for piece in range(SPLIT):
+            for way in ways:
+                if travels(way, step, half):
+                    ring(c, way, step, half, piece).wait_recv()
+                    if travels(way, step + 1, half):
+                        ring(c, way, step + 1, half, piece).start()
 
     qtile = rows // 2
 
@@ -224,14 +230,13 @@
 
     for kind, c, *rest in ORDER:
         if kind == BEGIN:
-            spread_done(((0, 1), (2, 3), (5, 6))[c][rest[0]])
+            spread_done(2 * c + rest[0])
             begin(c, rest[0])
         elif kind == QUERIES:
-            spread_done((4, 7)[c])
+            spread_done(6 + c)
         elif kind == PASS:
             step, half, way = rest
-            for one in (0, 1) if way == BOTH else (way,):
-                advance(c, step, half, one)
+            advance(c, step, half, (0, 1) if way == BOTH else (way,))
         else:
             attend(c, [lax.rem(blk + nx + rest[0], nx)])
 
@@ -414,8 +419,8 @@
         for step in range(1, hops + 1):
             for half in range(2):
                 for way in range(2):
-                    if travels(way, step, half):
-                        ring(c, way, step, half).wait_send()
+                    for piece in range(SPLIT if travels(way, step, half) else 0):
+                        ring(c, way, step, half, piece).wait_send()
 
 
 def local(
@@ -468,8 +473,8 @@
             pltpu.VMEM((8 * frames * COLS_DEV, wide), jnp.float32),
             pltpu.SemaphoreType.DMA((8,)),
             pltpu.SemaphoreType.DMA((8,)),
-            pltpu.SemaphoreType.DMA((3, 2, nx // 2, 2)),
-            pltpu.SemaphoreType.DMA((3, 2, nx // 2, 2)),
+            pltpu.SemaphoreType.DMA((3, 2, nx // 2, 2 * SPLIT)),
+            pltpu.SemaphoreType.DMA((3, 2, nx // 2, 2 * SPLIT)),
             pltpu.SemaphoreType.DMA,
             pltpu.SemaphoreType.DMA,
             pltpu.SemaphoreType.DMA((2, 2)),

time: 130 us -> 127 us (0.977)
  Pallas kernels: 128 us -> 125 us
    pallas_call x1, Pallas kernels: 128 us -> 125 us  [local(): pl.pallas_call(functools.partial(exchange_kernel, nz, nx), out_shape=jax....]
where the time goes in v1:
time: 127 us
  Pallas kernels  125 us (98%)
  other arithmetic  1.57 us (1%)
    pallas_call x1, Pallas kernels, local(): pl.pallas_call(functools.partial(exchange_kernel, nz, nx), out_shape=jax....  125 us

profile of v1, /device:TPU:65, one launch (start us, length us, event | category | flops | bytes accessed | tf_op | source)
XLA Modules:
  0.0 126.6 jit_solution(10879812122021296302)
XLA Ops:
  0.0 0.0 copy-start
  0.0 125.0 %shard_map.100 = f32[4,6,4,384]{3,2,1,0:T(4,128)} custom-call(bf16[48,4096]{1,0:T(8,128)(2,1)} %bitcast.11, bf16[48,4096]{1,0:T(8,128)(2,1)} %bitcast.12, bf16[48,4096]{1,0:T(8,128)(2,1)} %bitcast.13, bf16[64,4096]{1,0:T(8,128)(2,1)} %bitcast.10, bf16[432,384]{1,0:T(8,128)(2,1)} %bitcast.14, f32[48,64]{1,0:T(8,128)} %noisy_ref.1, s32[1,48]{1,0:T(1,128)} %bitcast.15, ...), custom_call_target="tpu_custom_call" | custom-call | tf_op jit(solution)/shard_map/pallas_call | solution.py:447
  125.0 0.0 copy-done
  125.0 1.6 %fusion = bf16[4,4,6,384]{3,1,2,0:T(4,128)(2,1)} fusion(f32[4,6,4,384]{3,2,1,0:T(4,128)} %shard_map.100, f32[384]{0:T(512)S(1)} %copy-done), kind=kLoop, calls=%fused_computation.1 | loop fusion | flops 73728 | bytes 222720 | tf_op jit(solution)/shard_map/transpose | solution.py:496
Async XLA Ops:
  0.0 125.0 %copy-start = (f32[384]{0:T(512)S(1)}, f32[384]{0:T(512)}, u32[]{:S(2)}) copy-start(f32[384]{0:T(512)} %param.19) | copy-start | bytes 4612

commit v2 on v1

--- a/solution.py
+++ b/solution.py
@@ -15,6 +15,7 @@
 TAP_LANES = 256
 ONES = 16
 SPLIT = 2
+VMEM_LIMIT = 55000 * 1024
 GUIDE = 5.0
 NOISE_LEVEL = 0.5
 MESH = pl.DeviceIdType.MESH
@@ -481,7 +482,9 @@
             pltpu.SemaphoreType.DMA((2,)),
             pltpu.SemaphoreType.DMA((5,)),
         ],
-        compiler_params=pltpu.CompilerParams(collective_id=0, has_side_effects=True),
+        compiler_params=pltpu.CompilerParams(
+            collective_id=0, has_side_effects=True, vmem_limit_bytes=VMEM_LIMIT
+        ),
     )(
         queries[0],
         key_states[0],

time: 127 us -> 126 us (level)
  local copies, waits for them, and re-layouts: 0.01 us -> 1.42 us
    unnamed x2 -> x10, local copies, waits for them, and re-layouts: 0.01 us -> 1.42 us
    pallas_call x1, Pallas kernels: 125 us -> 124 us  [local(): pl.pallas_call(functools.partial(exchange_kernel, nz, nx), out_shape=jax....]
where the time goes in v2:
time: 126 us
  Pallas kernels  124 us (98%)
  local copies, waits for them, and re-layouts  1.42 us (1%)
    pallas_call x1, Pallas kernels, local(): pl.pallas_call(functools.partial(exchange_kernel, nz, nx), out_shape=jax....  124 us

profile of v2, /device:TPU:65, one launch (start us, length us, event | category | flops | bytes accessed | tf_op | source)
XLA Modules:
  0.0 125.8 jit_solution(13666794947240076544)
XLA Ops:
  0.0 0.0 copy-start.1
  0.0 0.0 copy-start.2
  0.0 0.0 copy-start.3
  0.0 0.6 copy-done.1
  0.7 0.0 copy-done.2
  0.7 0.0 copy-done.3
  0.7 0.0 copy-start
  0.7 0.7 copy-done
  1.4 0.0 copy-start.4
  1.4 123.7 %shard_map.100 = f32[4,6,4,384]{3,2,1,0:T(4,128)S(1)} custom-call(bf16[48,4096]{1,0:T(8,128)(2,1)} %bitcast.14, bf16[48,4096]{1,0:T(8,128)(2,1)} %bitcast.15, bf16[48,4096]{1,0:T(8,128)(2,1)} %bitcast.16, bf16[64,4096]{1,0:T(8,128)(2,1)} %bitcast.13, bf16[432,384]{1,0:T(8,128)(2,1)} %bitcast.17, f32[48,64]{1,0:T(8,128)S(1)} %copy-done, ...), custom_call_target="tpu_custom_call" | custom-call | tf_op jit(solution)/shard_map/pallas_call | solution.py:448
  125.2 0.0 copy-done.4
  125.2 0.7 fusion
Async XLA Ops:
  0.0 0.7 copy-start.1
  0.0 0.7 copy-start.2
  0.0 0.7 copy-start.3
  0.7 0.7 copy-start
  1.4 123.7 %copy-start.4 = (f32[384]{0:T(512)S(1)}, f32[384]{0:T(512)}, u32[]{:S(2)}) copy-start(f32[384]{0:T(512)} %param.19) | copy-start | bytes 4612
